TPU v7x, 256 devices: a 4x2x16 block of a 4x16x16 slice. The times are simulated.
256 devices in a mesh: groups: 2 (over y), seq: 2 (over core), row: 16 (over z), col: 4 (over x).
Axes of the slice: x: 4, y: 2, z: 16, core: 2. Of those that a mesh axis runs over, the one named last changes fastest.
The devices are a block of a 4x16x16 slice.
Arguments:
- paired_left: bfloat16 [1024, 32, 512], P(('groups', 'seq', 'col'), None, 'row'), parts along dimension 0, may hold values from -24 to 24
- paired_right: bfloat16 [1024, 32, 512], P(('groups', 'seq', 'row'), None, 'col'), parts along dimension 0, may hold values from -24 to 24
- unpaired_left: bfloat16 [2048, 32, 512], P(('groups', 'seq', 'col'), None, 'row'), parts along dimension 0, may hold values from -24 to 24
- unpaired_right: bfloat16 [2048, 32, 512], P(('groups', 'seq', 'row'), None, 'col'), parts along dimension 0, may hold values from -24 to 24
- out_weight: bfloat16 [1024, 128], replicated, may hold values from -0.1875 to 0.1875
- out_bias: float32 [128], replicated, may hold values from -6 to 6
- chain_lengths: int32 [24], P('groups'), parts along dimension 0, may hold values from 1 to 128, 512 in all
- unpaired_depths: int32 [24], P('groups'), parts along dimension 0, may hold values from 256 to 1024
Outputs:
- pair_update: bfloat16 [1024, 512, 128], P(('groups', 'row'), ('col', 'seq')), parts along dimension 0
There are 2 independent parts, one for each index of `groups`. A program takes and returns all parts, laid end to end along the dimension named above; an argument that names none is the same for every part. Nothing has to cross between parts.
Inputs may be any that keep to these rules, and one draw needn't show every extreme that they name: `chain_lengths`: chain lengths sum to 512. `unpaired_depths`: rows of the unpaired MSA at or beyond a chain's depth are padding.
All inputs are finite; a program needn't handle non-finite values.
Results may differ from a plain program's by a relative error of at most 0.0034.
Values may be sent and summed in bfloat16 or wider, within the bound.
A program may use at most 64 MiB of HBM per device.

v0:
```python
import jax
import jax.numpy as jnp
from jax import lax
from jax.sharding import PartitionSpec as P

CHAINS = 12
S_P = 512


def in_order(blocks, dim):
    blocks = jnp.moveaxis(blocks, 0, dim)
    dims = blocks.shape
    return blocks.reshape(*dims[:dim], dims[dim] * dims[dim + 1], *dims[dim + 2 :])


def copy_for_each(shard, axis):
    devices = lax.axis_size(axis)
    return lax.all_to_all(
        jnp.broadcast_to(shard[None], (devices, *shard.shape)), axis, 0, 0, tiled=True
    )


def gathered_copies(shard, axis, dim):
    return in_order(copy_for_each(shard, axis), dim)


def gather_together(arrays, axis, dims):
    flat = jnp.concatenate([a.reshape(-1) for a in arrays])
    lines, at, gathered = (lax.all_gather(flat, axis), 0, [])
    for a, dim in zip(arrays, dims):
        blocks = lines[:, at : at + a.size].reshape(-1, *a.shape)
        gathered.append(in_order(blocks, dim))
        at += a.size
    return tuple(gathered)


def split_up(shard, dim, devices):
    dims = shard.shape
    blocks = shard.reshape(*dims[:dim], devices, dims[dim] // devices, *dims[dim + 1 :])
    return jnp.moveaxis(blocks, dim, 0)


def summed_on_arrival(shard, axis, dim):
    devices = lax.axis_size(axis)
    blocks = lax.all_to_all(split_up(shard, dim, devices), axis, 0, 0, tiled=True)
    return jnp.sum(blocks, axis=0)


def body(
    paired_left,
    paired_right,
    unpaired_left,
    unpaired_right,
    out_weight,
    out_bias,
    chain_lengths,
    unpaired_depths,
):
    left_pair, left_free = (
        gathered_copies(paired_left, "col", 0),
        gathered_copies(unpaired_left, "col", 0),
    )
    right_pair, right_free = gather_together((paired_right, unpaired_right), "row", (0, 0))
    rows_here = left_pair.shape[2]
    cols_here = right_pair.shape[2]
    first_row = lax.axis_index("row") * rows_here
    first_col = lax.axis_index("col") * cols_here
    residues = rows_here * lax.axis_size("row")
    positions = jnp.arange(residues, dtype=jnp.int32)
    chain_ends = jnp.cumsum(chain_lengths)
    chain_of = jnp.sum((positions[:, None] >= chain_ends[None, :]).astype(jnp.int32), axis=1)
    onehot = chain_of[:, None] == jnp.arange(CHAINS, dtype=jnp.int32)[None, :]
    depth_of = jnp.sum(jnp.where(onehot, unpaired_depths[None, :], 0), axis=1)
    chain_rows = lax.dynamic_slice_in_dim(chain_of, first_row, rows_here, 0)
    depth_rows = lax.dynamic_slice_in_dim(depth_of, first_row, rows_here, 0)
    chain_cols = lax.dynamic_slice_in_dim(chain_of, first_col, cols_here, 0)
    free_count = left_free.shape[0]
    free_ids = lax.axis_index("seq") * free_count + jnp.arange(free_count, dtype=jnp.int32)
    live_rows = (free_ids[:, None] < depth_rows[None, :]).astype(left_free.dtype)
    left_free = left_free * live_rows[:, None, :]
    same_chain = (chain_rows[:, None] == chain_cols[None, :]).astype(jnp.float32)
    block_rows = 4
    channels = out_weight.shape[1]

    def one_block(block_index):
        offset = block_index * block_rows
        left_block = lax.dynamic_slice_in_dim(left_pair, offset, block_rows, 2)
        free_block = lax.dynamic_slice_in_dim(left_free, offset, block_rows, 2)
        same_block = lax.dynamic_slice_in_dim(same_chain, offset, block_rows, 0)
        paired = jnp.einsum(
            "sci,sdj->ijcd", left_block, right_pair, preferred_element_type=jnp.float32
        )
        unpaired = jnp.einsum(
            "sci,sdj->ijcd", free_block, right_free, preferred_element_type=jnp.float32
        )
        unpaired = unpaired * same_block[:, :, None, None]
        outer_product = (paired + unpaired).astype(jnp.bfloat16).reshape(block_rows * cols_here, -1)
        projected = jnp.dot(outer_product, out_weight, preferred_element_type=jnp.float32)
        return projected.reshape(block_rows, cols_here, channels)

    projected = lax.map(one_block, jnp.arange(rows_here // block_rows, dtype=jnp.int32))
    projected = projected.reshape(rows_here, cols_here, channels)
    half_cols = cols_here // lax.axis_size("seq")
    own_offset = lax.axis_index("seq") * half_cols
    own_share = summed_on_arrival(projected, "seq", 1)
    same_share = lax.dynamic_slice_in_dim(same_chain, own_offset, half_cols, 1)
    denominator = S_P + same_share * depth_rows[:, None].astype(jnp.float32)
    return (own_share / denominator[:, :, None] + out_bias).astype(jnp.bfloat16)


def solution(mesh):
    return jax.shard_map(
        body,
        mesh=mesh,
        in_specs=(
            P(("groups", "seq", "col"), None, "row"),
            P(("groups", "seq", "row"), None, "col"),
            P(("groups", "seq", "col"), None, "row"),
            P(("groups", "seq", "row"), None, "col"),
            P(),
            P(),
            P("groups"),
            P("groups"),
        ),
        out_specs=P(("groups", "row"), ("col", "seq"), None),
        check_vma=False,
    )
```

profile of v0, /device:TPU:33, one launch (start us, length us, event | category | flops | bytes accessed | tf_op | source)
XLA Modules:
  0.0 197.5 jit_solution(5493444531071888708)
XLA Ops:
  6.6 1.7 pad_maximum_fusion
  8.4 1.1 copy.36
  9.6 1.6 reshape.100
  11.2 5.1 %all-to-all-start = ((bf16[4,2,32768]{2,1,0:T(2,128)(2,1)}), bf16[4,2,32768]{2,1,0:T(2,128)(2,1)S(1)}, u32[]{:S(2)}, u32[]{:S(2)}) async-start(bf16[4,2,32768]{2,1,0:T(2,128)(2,1)} %reshape.100), calls=%async_computation | async-start | bytes 1048576 | tf_op jit(solution)/shard_map/all_to_all | solution.py:18
  16.9 6.3 %all-to-all-done = bf16[4,2,32768]{2,1,0:T(2,128)(2,1)S(1)} async-done(((bf16[4,2,32768]{2,1,0:T(2,128)(2,1)}), bf16[4,2,32768]{2,1,0:T(2,128)(2,1)S(1)}, u32[]{:S(2)}, u32[]{:S(2)}) %all-to-all-start) | async-done | bytes 524320 | tf_op jit(solution)/shard_map/all_to_all | solution.py:18
  23.2 1.2 broadcast_in_dim.17
  24.4 3.6 %all-to-all-start.1 = ((bf16[4,128,32,32]{1,2,3,0:T(8,128)(2,1)}), bf16[4,128,32,32]{1,2,3,0:T(8,128)(2,1)S(1)}, u32[]{:S(2)}, u32[]{:S(2)}) async-start(bf16[4,128,32,32]{1,2,3,0:T(8,128)(2,1)} %broadcast_in_dim.17), calls=%async_computation.1 | async-start | bytes 2097152 | tf_op jit(solution)/shard_map/all_to_all | solution.py:18
  28.3 0.7 reshape.101
  29.0 0.8 copy.48
  29.8 1.5 reshape.99
  31.3 6.3 %all-to-all-done.1 = bf16[4,128,32,32]{1,2,3,0:T(8,128)(2,1)S(1)} async-done(((bf16[4,128,32,32]{1,2,3,0:T(8,128)(2,1)}), bf16[4,128,32,32]{1,2,3,0:T(8,128)(2,1)S(1)}, u32[]{:S(2)}, u32[]{:S(2)}) %all-to-all-start.1) | async-done | bytes 1048608 | tf_op jit(solution)/shard_map/all_to_all | solution.py:18
  37.6 0.8 copy.39
  38.4 0.4 reshape.90
  39.0 65.9 %all-gather.3.cloned.1.call-done = bf16[3145728]{0:T(1024)(128)(2,1)} async-done(((bf16[196608]{0:T(1024)(128)(2,1)}), bf16[3145728]{0:T(1024)(128)(2,1)}) %all-gather.3.cloned.1.call-update) | async-done | bytes 6291472 | tf_op jit(solution)/shard_map/all_gather | solution.py:29
  104.9 6.2 %reshape.93 = bf16[16,196608]{1,0:T(8,128)(2,1)} reshape(bf16[3145728]{0:T(1024)(128)(2,1)} %all-gather.3.cloned.1.call-done) | data formatting | bytes 12582912 | tf_op jit(solution)/shard_map/all_gather | solution.py:29
  111.1 4.4 %slice.9 = bf16[16,131072]{1,0:T(8,128)(2,1)} slice(bf16[16,196608]{1,0:T(8,128)(2,1)} %reshape.93), slice={[0:16], [65536:196608]} | slice | bytes 8388608 | tf_op jit(solution)/shard_map/slice | solution.py:31
  115.5 4.8 %reshape_reshape.10 = bf16[512,32,128]{2,1,0:T(8,128)(2,1)} reshape(bf16[16,131072]{1,0:T(8,128)(2,1)} %slice.9) | data formatting | bytes 8388608 | tf_op jit(solution)/shard_map/reshape;reshape | solution.py:13
  120.3 5.9 %copy.43 = bf16[512,32,128]{2,0,1:T(8,128)(2,1)} copy(bf16[512,32,128]{2,1,0:T(8,128)(2,1)} %reshape_reshape.10) | data formatting | bytes 8388608 | tf_op jit(solution)/shard_map/while | solution.py:101
  126.2 2.0 reshape_reshape.9
  128.1 2.4 %copy.41 = bf16[256,32,128]{2,0,1:T(8,128)(2,1)S(1)} copy(bf16[256,32,128]{2,1,0:T(8,128)(2,1)} %reshape_reshape.9) | data formatting | bytes 4194304 | tf_op jit(solution)/shard_map/while | solution.py:101
  130.6 47.4 %while.10 = (s32[]{:T(128)}, f32[8,4,128,128]{3,2,1,0:T(8,128)}, s32[8]{0:T(128)S(1)}, bf16[256,32,32]{0,1,2:T(8,128)(2,1)}, bf16[256,32,128]{2,0,1:T(8,128)(2,1...) while((s32[]{:T(128)}, f32[8,4,128,128]{3,2,1,0:T(8,128)}, ...), condition=%wide.region_4.5_spmd, body=%wide.region_3.4_spmd.sunk | while | flops 941096960 | bytes 32446700 | solution.py:101
  130.6 0.6 dynamic_slice.44
  132.0 1.4 fusion.29
  133.4 0.8 copy-done.1
  134.2 0.8 fusion.30
  135.4 1.2 fusion.31
  136.6 0.6 dynamic_slice.44
  137.9 1.4 fusion.29
  139.4 0.8 copy-done.1
  140.1 0.8 fusion.30
  141.3 1.2 fusion.31
  142.5 0.6 dynamic_slice.44
  143.8 1.4 fusion.29
  145.3 0.8 copy-done.1
  146.0 0.8 fusion.30
  147.2 1.2 fusion.31
  148.4 0.6 dynamic_slice.44
  149.8 1.4 fusion.29
  151.2 0.8 copy-done.1
  152.0 0.8 fusion.30
  153.2 1.2 fusion.31
  154.3 0.6 dynamic_slice.44
  155.7 1.4 fusion.29
  157.1 0.8 copy-done.1
  157.9 0.8 fusion.30
  159.1 1.2 fusion.31
  160.3 0.6 dynamic_slice.44
  161.6 1.4 fusion.29
  163.1 0.8 copy-done.1
  163.8 0.8 fusion.30
  165.0 1.2 fusion.31
  166.2 0.6 dynamic_slice.44
  167.6 1.4 fusion.29
  169.0 0.8 copy-done.1
  169.8 0.8 fusion.30
  171.0 1.2 fusion.31
  172.1 0.6 dynamic_slice.44
  173.5 1.4 fusion.29
  174.9 0.8 copy-done.1
  175.7 0.8 fusion.30
  176.9 1.2 fusion.31
  178.0 1.7 copy.44
  179.8 9.1 %all_to_all.15 = f32[2,32,64,128]{3,2,1,0:T(8,128)S(1)} all-to-all(f32[2,32,64,128]{3,2,1,0:T(8,128)S(1)} %copy.44), channel_id=1, replica_groups=mesh['groups'=2,'seq'=2,'row'=16,'col'=4] {'seq'}, dimensions={0} | all-to-all | bytes 4194304 | tf_op jit(solution)/shard_map/all_to_all | solution.py:45
  189.5 1.1 add_convert_fusion.1
  (62 shorter events, 5.9 us)
Async XLA Ops:
  6.5 98.3 %all-gather.3.cloned.1.call-start = ((), (), s32[]{:S(2)}) async-start(), calls=%async_computation.3 | async-start | bytes 6684672 | tf_op jit(solution)/shard_map/all_gather | solution.py:29
  9.4 6.9 %copy-start.5 = (s32[12]{0:T(128)S(1)}, s32[12]{0:T(128)}, u32[]{:S(2)}) copy-start(s32[12]{0:T(128)} %param.16) | copy-start | bytes 148
  9.4 7.0 %copy-start.2 = (bf16[128,32,32]{0,2,1:T(8,128)(2,1)S(1)}, bf16[128,32,32]{0,2,1:T(8,128)(2,1)}, u32[]{:S(2)}) copy-start(bf16[128,32,32]{0,2,1:T(8,128)(2,1)} %param.12) | copy-start | bytes 786436
  9.4 7.3 %copy-start.4 = (s32[12]{0:T(128)S(1)}, s32[12]{0:T(128)}, u32[]{:S(2)}) copy-start(s32[12]{0:T(128)} %param.17) | copy-start | bytes 148
  11.2 12.1 %all-to-all-start = ((bf16[4,2,32768]{2,1,0:T(2,128)(2,1)}), bf16[4,2,32768]{2,1,0:T(2,128)(2,1)S(1)}, u32[]{:S(2)}, u32[]{:S(2)}) async-start(bf16[4,2,32768]{2,1,0:T(2,128)(2,1)} %reshape.100), calls=%async_computation | async-start | bytes 1048576 | tf_op jit(solution)/shard_map/all_to_all | solution.py:18
  24.4 13.3 %all-to-all-start.1 = ((bf16[4,128,32,32]{1,2,3,0:T(8,128)(2,1)}), bf16[4,128,32,32]{1,2,3,0:T(8,128)(2,1)S(1)}, u32[]{:S(2)}, u32[]{:S(2)}) async-start(bf16[4,128,32,32]{1,2,3,0:T(8,128)(2,1)} %broadcast_in_dim.17), calls=%async_computation.1 | async-start | bytes 2097152 | tf_op jit(solution)/shard_map/all_to_all | solution.py:18
  120.3 5.9 %slice-start = ((bf16[16,196608]{1,0:T(8,128)(2,1)}), bf16[16,65536]{1,0:T(8,128)(2,1)S(1)}, s32[]{:S(2)}) async-start(bf16[16,196608]{1,0:T(8,128)(2,1)} %reshape.93), calls=%async_computation.4 | async-start | bytes 4194304 | tf_op jit(solution)/shard_map/slice | solution.py:31
  128.1 2.5 %copy-start = (bf16[1024,128]{1,0:T(8,128)(2,1)S(1)}, bf16[1024,128]{1,0:T(8,128)(2,1)}, u32[]{:S(2)}) copy-start(bf16[1024,128]{1,0:T(8,128)(2,1)} %param.14) | copy-start | bytes 786436
  132.0 2.2 %copy-start.1 = (bf16[512,32,128]{2,0,1:T(8,128)(2,1)S(1)}, bf16[512,32,128]{2,0,1:T(8,128)(2,1)}, u32[]{:S(2)}) copy-start(bf16[512,32,128]{2,0,1:T(8,128)(2,1)} %get-tuple-element.196) | copy-start | bytes 12582916 | tf_op jit(solution)/shard_map/while
  137.9 2.2 %copy-start.1 = (bf16[512,32,128]{2,0,1:T(8,128)(2,1)S(1)}, bf16[512,32,128]{2,0,1:T(8,128)(2,1)}, u32[]{:S(2)}) copy-start(bf16[512,32,128]{2,0,1:T(8,128)(2,1)} %get-tuple-element.196) | copy-start | bytes 12582916 | tf_op jit(solution)/shard_map/while
  143.8 2.2 %copy-start.1 = (bf16[512,32,128]{2,0,1:T(8,128)(2,1)S(1)}, bf16[512,32,128]{2,0,1:T(8,128)(2,1)}, u32[]{:S(2)}) copy-start(bf16[512,32,128]{2,0,1:T(8,128)(2,1)} %get-tuple-element.196) | copy-start | bytes 12582916 | tf_op jit(solution)/shard_map/while
  149.8 2.2 %copy-start.1 = (bf16[512,32,128]{2,0,1:T(8,128)(2,1)S(1)}, bf16[512,32,128]{2,0,1:T(8,128)(2,1)}, u32[]{:S(2)}) copy-start(bf16[512,32,128]{2,0,1:T(8,128)(2,1)} %get-tuple-element.196) | copy-start | bytes 12582916 | tf_op jit(solution)/shard_map/while
  155.7 2.2 %copy-start.1 = (bf16[512,32,128]{2,0,1:T(8,128)(2,1)S(1)}, bf16[512,32,128]{2,0,1:T(8,128)(2,1)}, u32[]{:S(2)}) copy-start(bf16[512,32,128]{2,0,1:T(8,128)(2,1)} %get-tuple-element.196) | copy-start | bytes 12582916 | tf_op jit(solution)/shard_map/while
  161.6 2.2 %copy-start.1 = (bf16[512,32,128]{2,0,1:T(8,128)(2,1)S(1)}, bf16[512,32,128]{2,0,1:T(8,128)(2,1)}, u32[]{:S(2)}) copy-start(bf16[512,32,128]{2,0,1:T(8,128)(2,1)} %get-tuple-element.196) | copy-start | bytes 12582916 | tf_op jit(solution)/shard_map/while
  167.5 2.2 %copy-start.1 = (bf16[512,32,128]{2,0,1:T(8,128)(2,1)S(1)}, bf16[512,32,128]{2,0,1:T(8,128)(2,1)}, u32[]{:S(2)}) copy-start(bf16[512,32,128]{2,0,1:T(8,128)(2,1)} %get-tuple-element.196) | copy-start | bytes 12582916 | tf_op jit(solution)/shard_map/while
  173.5 2.2 %copy-start.1 = (bf16[512,32,128]{2,0,1:T(8,128)(2,1)S(1)}, bf16[512,32,128]{2,0,1:T(8,128)(2,1)}, u32[]{:S(2)}) copy-start(bf16[512,32,128]{2,0,1:T(8,128)(2,1)} %get-tuple-element.196) | copy-start | bytes 12582916 | tf_op jit(solution)/shard_map/while
  188.9 0.7 copy-start.3
Sparse Core Ops, SparseCore 0:
  9.1 95.6 all-gather.2
where the time goes:
time: 198 us
  waiting for transfers between devices  78.6 us (40%)
  local copies, waits for them, and re-layouts  51.3 us (26%)
  matrix products  27.1 us (14%)
  between operations  13.5 us (7%)
  blocking collectives  9.09 us (5%)
  starting transfers between devices  8.72 us (4%)
  loops' own time  5.3 us (3%)
  other arithmetic  3.86 us (2%)
    all_gather x1, waiting for transfers between devices, gather_together(): lines, at, gathered = (lax.all_gather(flat, axis), 0, [])  65.9 us
    all_to_all x2, waiting for transfers between devices, copy_for_each(): lax.all_to_all(jnp.broadcast_to(shard[None], (devices, *shard.shape)), ax...  12.6 us
    dot_general x8, matrix products, one_block(): jnp.einsum('sci,sdj->ijcd', left_block, right_pair, preferred_element_typ...  11.6 us
    while x4, local copies, waits for them, and re-layouts, body(): lax.map(one_block, jnp.arange(rows_here // block_rows, dtype=jnp.int32))  10.6 us
    dot_general x8, matrix products, one_block(): jnp.dot(outer_product, out_weight, preferred_element_type=jnp.float32)  9.43 us
    all_to_all x1, blocking collectives, summed_on_arrival(): lax.all_to_all(split_up(shard, dim, devices), axis, 0, 0, tiled=True)  9.09 us
    all_to_all x2, starting transfers between devices, copy_for_each(): lax.all_to_all(jnp.broadcast_to(shard[None], (devices, *shard.shape)), ax...  8.72 us
    another operation x2, local copies, waits for them, and re-layouts, in_order(): blocks.reshape(*dims[:dim], dims[dim] * dims[dim + 1], *dims[dim + 2:])  6.79 us
  transfers between devices with their start and end apart: 3, of which 3 were waited for; matrix products, arithmetic and copies ran while one was open for 5% of the time, Pallas kernels for 0%

commit v1 on v0

v1 whole, which is shorter than its diff:
```python
import functools

import jax
import jax.numpy as jnp
from jax import lax
from jax.experimental import pallas as pl
from jax.experimental.pallas import tpu as pltpu
from jax.sharding import PartitionSpec as P

MESH = pl.DeviceIdType.MESH
F32 = jnp.float32
BF16 = jnp.bfloat16
PHASES = 4
ROWS_PER_UNIT = 4


def kernel(
    dims,
    rp_ref,
    ru_ref,
    lp_ref,
    lu_ref,
    wt_ref,
    bias_ref,
    len_ref,
    dep_ref,
    out_ref,
    rbp,
    rbu,
    lbp,
    lbu,
    ltp,
    ltu,
    acc,
    part,
    got,
    same_ref,
    scale_ref,
    send_r,
    recv_r,
    send_l,
    recv_l,
    send_x,
    recv_x,
):
    nrow, ncol, nseq, chans, chains, ni, nj, nz, s_paired = dims
    me = lax.axis_index("row")
    col = lax.axis_index("col")
    seq = lax.axis_index("seq")
    right, left = lax.rem(me + 1, nrow), lax.rem(me + nrow - 1, nrow)
    other = 1 - seq
    lanes = chans * nj // PHASES
    per_phase = chans // PHASES

    barrier = pltpu.get_barrier_semaphore()
    for nb in (right, left):
        pl.semaphore_signal(barrier, inc=1, device_id={"row": nb}, device_id_type=MESH)
    for k in range(1, ncol):
        pl.semaphore_signal(
            barrier, inc=1, device_id={"col": lax.rem(col + k, ncol)}, device_id_type=MESH
        )
    pl.semaphore_signal(barrier, inc=1, device_id={"seq": other}, device_id_type=MESH)
    pl.semaphore_wait(barrier, 2 + ncol - 1 + 1)

    half = nrow // 2

    def steps(way, ph):
        return half if (ph + way) % 2 == 0 else half - 1

    def block(way, t):
        return lax.rem(me - t + nrow, nrow) if way == 0 else lax.rem(me + t, nrow)

    def ring(way, ph, t, kind):
        q = block(way, t - 1)
        buf, own = ((rbp, rp_ref), (rbu, ru_ref))[kind]
        part_of = pl.ds(ph * lanes, lanes)
        src = own.at[:, part_of] if t == 1 else buf.at[q, :, part_of]
        at = ((way * PHASES + ph) * half + t - 1) * 2 + kind
        return pltpu.make_async_remote_copy(
            src_ref=src,
            dst_ref=buf.at[q, :, part_of],
            send_sem=send_r.at[at],
            recv_sem=recv_r.at[at],
            device_id={"row": right if way == 0 else left},
            device_id_type=MESH,
        )

    def arrival(way, ph, t, kind):
        q = block(way, t)
        buf = (rbp, rbu)[kind]
        part_of = pl.ds(ph * lanes, lanes)
        at = ((way * PHASES + ph) * half + t - 1) * 2 + kind
        return pltpu.make_async_remote_copy(
            src_ref=buf.at[q, :, part_of],
            dst_ref=buf.at[q, :, part_of],
            send_sem=send_r.at[at],
            recv_sem=recv_r.at[at],
            device_id={"row": right if way == 0 else left},
            device_id_type=MESH,
        )

    def first_sends(phases):
        for kind in (1, 0):
            for ph in phases:
                for way in (0, 1):
                    ring(way, ph, 1, kind).start()

    def left_copy(k, kind, incoming):
        own, buf = ((lp_ref, lbp), (lu_ref, lbu))[kind]
        at = (k - 1) * 2 + kind
        slot = lax.rem(col - k + ncol, ncol) if incoming else col
        return pltpu.make_async_remote_copy(
            src_ref=own,
            dst_ref=buf.at[slot],
            send_sem=send_l.at[at],
            recv_sem=recv_l.at[at],
            device_id={"col": lax.rem(col + k, ncol)},
            device_id_type=MESH,
        )

    first_sends((0, 1))
    for k in range(1, ncol):
        for kind in (0, 1):
            left_copy(k, kind, False).start()

    rbp[pl.ds(me, 1)] = rp_ref[...][None]
    rbu[pl.ds(me, 1)] = ru_ref[...][None]
    lbp[pl.ds(col, 1)] = lp_ref[...][None]
    lbu[pl.ds(col, 1)] = lu_ref[...][None]
    acc[...] = jnp.zeros_like(acc)

    pos_i = lax.broadcasted_iota(jnp.int32, (ni, nj), 0) + me * ni
    pos_j = lax.broadcasted_iota(jnp.int32, (ni, nj), 1) + col * nj
    chain_i = jnp.zeros((ni, nj), jnp.int32)
    chain_j = jnp.zeros((ni, nj), jnp.int32)
    end = jnp.int32(0)
    ends = []
    for k in range(chains):
        end = end + len_ref[k]
        ends.append(end)
        chain_i = chain_i + (pos_i >= end).astype(jnp.int32)
        chain_j = chain_j + (pos_j >= end).astype(jnp.int32)
    same = (chain_i == chain_j).astype(F32)
    depth_i = jnp.zeros((ni, nj), F32)
    for k in range(chains):
        depth_i = depth_i + jnp.where(chain_i == k, dep_ref[k].astype(F32), 0.0)
    same_ref[...] = same
    scale_ref[...] = 1.0 / (s_paired + same * depth_i)

    def forward(ph, t):
        for kind in (1, 0):
            for way in (0, 1):
                if t <= steps(way, ph):
                    arrival(way, ph, t, kind).wait_recv()
                    if t < steps(way, ph):
                        ring(way, ph, t + 1, kind).start()

    free_rows = lbu.shape[0] * lbu.shape[1]
    block_rows = 128

    def left_ready():
        for k in range(1, ncol):
            for kind in (0, 1):
                left_copy(k, kind, True).wait_recv()
        ltp[...] = lbp[...].reshape(-1, ni * chans).T
        ltu[...] = lbu[...].reshape(-1, ni * chans).T

        def mask_rows(b, _):
            rows = pl.ds(pl.multiple_of(b * block_rows, block_rows), block_rows)
            shape = (block_rows, free_rows)
            pos = (lax.broadcasted_iota(jnp.int32, shape, 0) + b * block_rows) // chans + me * ni
            ids = lax.broadcasted_iota(jnp.int32, shape, 1) + seq * free_rows
            depth = jnp.zeros(shape, jnp.int32)
            for k in range(chains):
                low = ends[k - 1] if k else 0
                depth = jnp.where((pos >= low) & (pos < ends[k]), dep_ref[k], depth)
            live = jnp.where(ids < depth, 1.0, 0.0).astype(BF16)
            ltu[rows, :] = ltu[rows, :] * live
            return 0

        lax.fori_loop(0, ni * chans // block_rows, mask_rows, 0)

    def unit(ph, ib):
        rows = ROWS_PER_UNIT * chans
        at = pl.ds(pl.multiple_of(ib * rows, rows), rows)
        part_of = pl.ds(ph * lanes, lanes)
        kp = rbp.shape[0] * rbp.shape[1]
        ku = rbu.shape[0] * rbu.shape[1]
        a = jnp.dot(ltp[at, :], rbp[:, :, part_of].reshape(kp, lanes), preferred_element_type=F32)
        b = jnp.dot(ltu[at, :], rbu[:, :, part_of].reshape(ku, lanes), preferred_element_type=F32)
        w = wt_ref[:, ph * per_phase * chans : (ph + 1) * per_phase * chans]
        for pair in range(ROWS_PER_UNIT // 2):
            cols = []
            for ii in (2 * pair, 2 * pair + 1):
                m = same_ref[pl.ds(ib * ROWS_PER_UNIT + ii, 1), :]
                tiles = []
                for d in range(per_phase):
                    rs = slice(ii * chans, (ii + 1) * chans)
                    ls = slice(d * nj, (d + 1) * nj)
                    tiles.append((a[rs, ls] + b[rs, ls] * m).astype(BF16))
                cols.append(jnp.concatenate(tiles, axis=0))
            x = jnp.concatenate(cols, axis=1)
            to = pl.ds(pl.multiple_of((ib * ROWS_PER_UNIT + 2 * pair) * nj, 2 * nj), 2 * nj)
            acc[:, to] += jnp.dot(w, x, preferred_element_type=F32)

    units = ni // ROWS_PER_UNIT
    for t in range(1, half + 1):
        for ph in (0, 1):
            forward(ph, t)
            if t == half:
                pass
        if t == half - 1:
            first_sends((2, 3))
        if t == half // 2:
            left_ready()
    for t in range(1, half + 1):
        for ph in (2, 3):
            forward(ph, t)

        def two(n, _, t=t):
            unit(0, n + (t - 1))
            unit(1, n + (t - 1))
            return 0

        lax.fori_loop(0, 1, two, 0)

    def tail(n, _):
        unit(2, n)
        unit(3, n)
        return 0

    lax.fori_loop(0, units, tail, 0)

    def turn(i, _):
        tile = acc[:, pl.ds(pl.multiple_of(i * nj, nj), nj)] * scale_ref[pl.ds(i, 1), :]
        part[pl.ds(i, 1)] = tile.T[None]
        return 0

    lax.fori_loop(0, ni, turn, 0)
    hj = nj // nseq
    swap = pltpu.make_async_remote_copy(
        src_ref=part.at[:, pl.ds(pl.multiple_of(other * hj, hj), hj), :],
        dst_ref=got,
        send_sem=send_x,
        recv_sem=recv_x,
        device_id={"seq": other},
        device_id_type=MESH,
    )
    swap.start()
    swap.wait_recv()

    def finish(i, _):
        mine = part[pl.ds(i, 1), pl.ds(pl.multiple_of(seq * hj, hj), hj), :]
        out_ref[pl.ds(i, 1)] = (mine + got[pl.ds(i, 1)] + bias_ref[...][None]).astype(BF16)
        return 0

    lax.fori_loop(0, ni, finish, 0)

    swap.wait_send()
    for k in range(1, ncol):
        for kind in (0, 1):
            left_copy(k, kind, False).wait_send()
    for ph in range(PHASES):
        for way in (0, 1):
            for t in range(1, steps(way, ph) + 1):
                for kind in (0, 1):
                    ring(way, ph, t, kind).wait_send()


def body(sizes, pl_, pr, ul, ur, weight, bias, lengths, depths):
    nrow, ncol, nseq = sizes
    chans, ni = pl_.shape[1], pl_.shape[2]
    nj = pr.shape[2]
    nz = weight.shape[1]
    rp = pr.reshape(pr.shape[0], chans * nj)
    ru = ur.reshape(ur.shape[0], chans * nj)
    lp = jnp.transpose(pl_, (0, 2, 1)).reshape(pl_.shape[0], ni * chans)
    lu = jnp.transpose(ul, (0, 2, 1)).reshape(ul.shape[0], ni * chans)
    wt = jnp.transpose(weight.reshape(chans, chans, nz), (2, 1, 0)).reshape(nz, chans * chans)
    s_paired = float(pr.shape[0] * nrow * nseq)
    dims = (nrow, ncol, nseq, chans, lengths.shape[0], ni, nj, nz, s_paired)
    half = nrow // 2
    vm = pl.BlockSpec(memory_space=pltpu.VMEM)
    sm = pl.BlockSpec(memory_space=pltpu.SMEM)
    dma = pltpu.SemaphoreType.DMA
    hj = nj // nseq
    return pl.pallas_call(
        functools.partial(kernel, dims),
        out_shape=jax.ShapeDtypeStruct((ni, hj, nz), BF16),
        in_specs=[vm] * 6 + [sm] * 2,
        out_specs=vm,
        scratch_shapes=[
            pltpu.VMEM((nrow, pr.shape[0], chans * nj), BF16),
            pltpu.VMEM((nrow, ur.shape[0], chans * nj), BF16),
            pltpu.VMEM((ncol, *lp.shape), BF16),
            pltpu.VMEM((ncol, *lu.shape), BF16),
            pltpu.VMEM((ni * chans, ncol * lp.shape[0]), BF16),
            pltpu.VMEM((ni * chans, ncol * lu.shape[0]), BF16),
            pltpu.VMEM((nz, ni * nj), F32),
            pltpu.VMEM((ni, nj, nz), F32),
            pltpu.VMEM((ni, hj, nz), F32),
            pltpu.VMEM((ni, nj), F32),
            pltpu.VMEM((ni, nj), F32),
            dma((2 * PHASES * half * 2,)),
            dma((2 * PHASES * half * 2,)),
            dma(((ncol - 1) * 2,)),
            dma(((ncol - 1) * 2,)),
            dma,
            dma,
        ],
        compiler_params=pltpu.CompilerParams(
            collective_id=0, has_side_effects=True, vmem_limit_bytes=48 * 1024 * 1024
        ),
    )(rp, ru, lp, lu, wt, bias.reshape(1, nz), lengths, depths)


def solution(mesh):
    sizes = (mesh.shape["row"], mesh.shape["col"], mesh.shape["seq"])
    return jax.shard_map(
        functools.partial(body, sizes),
        mesh=mesh,
        in_specs=(
            P(("groups", "seq", "col"), None, "row"),
            P(("groups", "seq", "row"), None, "col"),
            P(("groups", "seq", "col"), None, "row"),
            P(("groups", "seq", "row"), None, "col"),
            P(),
            P(),
            P("groups"),
            P("groups"),
        ),
        out_specs=P(("groups", "row"), ("col", "seq"), None),
        check_vma=False,
    )
```

time: 198 us -> 118 us (0.60)
  Pallas kernels: 0 us -> 112 us
  waiting for transfers between devices: 78.6 us -> 0 us
  local copies, waits for them, and re-layouts: 51.3 us -> 5.6 us
  matrix products: 27.1 us -> 0 us
  between operations: 13.5 us -> 0.09 us
  blocking collectives: 9.09 us -> 0 us
  starting transfers between devices: 8.72 us -> 0 us
  loops' own time: 5.3 us -> 0 us
  other arithmetic: 3.86 us -> 0 us
    pallas_call x0 -> x1, Pallas kernels: none -> 112 us  [body(): pl.pallas_call(functools.partial(kernel, dims), out_shape=jax.ShapeDtypeS...]
    all_gather x1 -> x0, waiting for transfers between devices: 65.9 us -> none  [gather_together(): lines, at, gathered = (lax.all_gather(flat, axis), 0, [])]
    dot_general x24 -> x0, matrix products: 27.1 us -> none  [the longest x8 11.6 us: one_block(): jnp.einsum('sci,sdj->ijcd', left_block, right_pair, preferred_element_typ...]
    while x20 -> x0, local copies, waits for them, and re-layouts: 16.7 us -> none  [the longest x4 10.6 us: body(): lax.map(one_block, jnp.arange(rows_here // block_rows, dtype=jnp.int32))]
    all_to_all x2 -> x0, waiting for transfers between devices: 12.6 us -> none  [copy_for_each(): lax.all_to_all(jnp.broadcast_to(shard[None], (devices, *shard.shape)), ax...]
    all_to_all x1 -> x0, blocking collectives: 9.09 us -> none  [summed_on_arrival(): lax.all_to_all(split_up(shard, dim, devices), axis, 0, 0, tiled=True)]
    all_to_all x2 -> x0, starting transfers between devices: 8.72 us -> none  [copy_for_each(): lax.all_to_all(jnp.broadcast_to(shard[None], (devices, *shard.shape)), ax...]
    another operation x2 -> x0, local copies, waits for them, and re-layouts: 6.79 us -> none  [in_order(): blocks.reshape(*dims[:dim], dims[dim] * dims[dim + 1], *dims[dim + 2:])]
  transfers between devices with their start and end apart: 3 -> 0, of which waited for: 3 -> 0; matrix products, arithmetic and copies ran while one was open for 5% -> 0% of each run, Pallas kernels for 0% -> 0%
where the time goes in v1:
time: 118 us
  Pallas kernels  112 us (95%)
  local copies, waits for them, and re-layouts  5.6 us (5%)
    pallas_call x1, Pallas kernels, body(): pl.pallas_call(functools.partial(kernel, dims), out_shape=jax.ShapeDtypeS...  112 us
    unnamed x18, local copies, waits for them, and re-layouts  4.97 us

profile of v1, /device:TPU:33, one launch (start us, length us, event | category | flops | bytes accessed | tf_op | source)
XLA Modules:
  0.0 117.7 jit_solution(3018089405264576391)
XLA Ops:
  0.0 0.0 copy-start.3
  0.0 1.0 copy.28
  1.0 0.0 copy-done.3
  1.0 0.1 copy.17
  1.1 0.0 copy-start.4
  1.1 0.1 copy.20.lp_ref
  1.3 0.8 copy-done.4
  2.1 0.1 copy.18
  2.2 0.0 copy-start.5
  2.2 0.1 copy.21.lu_ref
  2.4 0.8 copy-done.5
  3.1 0.0 copy-start.6
  3.1 0.1 copy.27
  3.3 0.8 copy-done.6
  4.1 0.1 copy.19
  4.2 0.0 copy-start
  4.2 0.0 copy-start.1
  4.2 0.0 copy-start.2
  4.2 0.1 copy.22.wt_ref
  4.4 0.5 copy-done
  4.9 0.0 copy-done.1
  4.9 0.0 copy-done.2
  4.9 112.0 %shard_map.82 = bf16[32,64,128]{2,1,0:T(8,128)(2,1)S(1)} custom-call(bf16[16,4096]{1,0:T(8,128)(2,1)S(1)} %bitcast.19, bf16[32,4096]{1,0:T(8,128)(2,1)S(1)} %bitcast.18, bf16[64,1024]{1,0:T(8,128)(2,1)S(1)} %copy.20.lp_ref, bf16[128,1024]{1,0:T(8,128)(2,1)S(1)} %copy.21.lu_ref, bf16[128,1024]{1,0:T(8,128)(2,1)S(1)} %copy.22.wt_ref, f32[1,128]{1,0:T(1,128)S(1)} %bitcast.20, ...), custom_call_target="tpu_custom_call" | custom-call | tf_op jit(solution)/shard_map/pallas_call | solution.py:287
  116.9 0.8 copy.30
Async XLA Ops:
  0.0 1.0 copy-start.3
  1.1 1.0 copy-start.4
  2.2 1.0 copy-start.5
  3.1 0.9 copy-start.6
  4.2 0.7 copy-start
  4.2 0.7 copy-start.1
  4.2 0.7 copy-start.2

commit v2 on v1

--- a/solution.py
+++ b/solution.py
@@ -12,23 +12,30 @@
 BF16 = jnp.bfloat16
 PHASES = 4
 ROWS_PER_UNIT = 4
+STAGGER = 2
 
 
 def kernel(
     dims,
-    rp_ref,
-    ru_ref,
-    lp_ref,
-    lu_ref,
-    wt_ref,
+    pr_ref,
+    ur_ref,
+    pl_ref,
+    ul_ref,
+    w_ref,
     bias_ref,
     len_ref,
     dep_ref,
     out_ref,
+    prv,
+    urv,
+    plv,
+    ulv,
+    wv,
+    perm,
+    wt_ref,
     rbp,
     rbu,
     lbp,
-    lbu,
     ltp,
     ltu,
     acc,
@@ -42,6 +49,7 @@
     recv_l,
     send_x,
     recv_x,
+    load_sem,
 ):
     nrow, ncol, nseq, chans, chains, ni, nj, nz, s_paired = dims
     me = lax.axis_index("row")
@@ -52,6 +60,15 @@
     lanes = chans * nj // PHASES
     per_phase = chans // PHASES
 
+    loads = [
+        pltpu.make_async_copy(src, dst, load_sem.at[k])
+        for k, (src, dst) in enumerate(
+            ((pr_ref, prv), (ur_ref, urv), (pl_ref, plv), (ul_ref, ulv), (w_ref, wv))
+        )
+    ]
+    for load in loads:
+        load.start()
+
     barrier = pltpu.get_barrier_semaphore()
     for nb in (right, left):
         pl.semaphore_signal(barrier, inc=1, device_id={"row": nb}, device_id_type=MESH)
@@ -60,6 +77,10 @@
             barrier, inc=1, device_id={"col": lax.rem(col + k, ncol)}, device_id_type=MESH
         )
     pl.semaphore_signal(barrier, inc=1, device_id={"seq": other}, device_id_type=MESH)
+    loads[0].wait()
+    rbp[pl.ds(me, 1)] = prv[...].reshape(1, -1, chans * nj)
+    loads[1].wait()
+    rbu[pl.ds(me, 1)] = urv[...].reshape(1, -1, chans * nj)
     pl.semaphore_wait(barrier, 2 + ncol - 1 + 1)
 
     half = nrow // 2
@@ -72,12 +93,11 @@
 
     def ring(way, ph, t, kind):
         q = block(way, t - 1)
-        buf, own = ((rbp, rp_ref), (rbu, ru_ref))[kind]
+        buf = (rbp, rbu)[kind]
         part_of = pl.ds(ph * lanes, lanes)
-        src = own.at[:, part_of] if t == 1 else buf.at[q, :, part_of]
         at = ((way * PHASES + ph) * half + t - 1) * 2 + kind
         return pltpu.make_async_remote_copy(
-            src_ref=src,
+            src_ref=buf.at[q, :, part_of],
             dst_ref=buf.at[q, :, part_of],
             send_sem=send_r.at[at],
             recv_sem=recv_r.at[at],
@@ -99,34 +119,56 @@
             device_id_type=MESH,
         )
 
-    def first_sends(phases):
+    def first_sends(ph):
         for kind in (1, 0):
-            for ph in phases:
-                for way in (0, 1):
-                    ring(way, ph, 1, kind).start()
+            for way in (0, 1):
+                ring(way, ph, 1, kind).start()
+
+    tall = ni * chans
+    lu_rows = ulv.shape[2]
 
     def left_copy(k, kind, incoming):
-        own, buf = ((lp_ref, lbp), (lu_ref, lbu))[kind]
         at = (k - 1) * 2 + kind
         slot = lax.rem(col - k + ncol, ncol) if incoming else col
+        if kind == 0:
+            src = dst = lbp.at[slot]
+        else:
+            src = dst = ltu.at[:, pl.ds(pl.multiple_of(slot * lu_rows, lu_rows), lu_rows)]
         return pltpu.make_async_remote_copy(
-            src_ref=own,
-            dst_ref=buf.at[slot],
+            src_ref=src,
+            dst_ref=dst,
             send_sem=send_l.at[at],
             recv_sem=recv_l.at[at],
             device_id={"col": lax.rem(col + k, ncol)},
             device_id_type=MESH,
         )
 
-    first_sends((0, 1))
+    first_sends(0)
+
+    block_rows = 128
+
+    def fill(b, _):
+        rows = pl.ds(pl.multiple_of(b * block_rows, block_rows), block_rows)
+        r = lax.broadcasted_iota(jnp.int32, (block_rows, tall), 0) + b * block_rows
+        k = lax.broadcasted_iota(jnp.int32, (block_rows, tall), 1)
+        hit = k == (r % chans) * chans + r // chans
+        perm[rows, :] = jnp.where(hit, 1.0, 0.0).astype(BF16)
+        return 0
+
+    lax.fori_loop(0, tall // block_rows, fill, 0)
+    for load in loads[2:]:
+        load.wait()
+    lbp[pl.ds(col, 1)] = lax.dot_general(
+        plv[...].reshape(tall, -1), perm[...], (((0,), (1,)), ((), ())),
+        preferred_element_type=F32,
+    ).astype(BF16)[None]
+    ltu[:, pl.ds(pl.multiple_of(col * lu_rows, lu_rows), lu_rows)] = jnp.dot(
+        perm[...], ulv[...].reshape(tall, -1), preferred_element_type=F32
+    ).astype(BF16)
     for k in range(1, ncol):
         for kind in (0, 1):
             left_copy(k, kind, False).start()
-
-    rbp[pl.ds(me, 1)] = rp_ref[...][None]
-    rbu[pl.ds(me, 1)] = ru_ref[...][None]
-    lbp[pl.ds(col, 1)] = lp_ref[...][None]
-    lbu[pl.ds(col, 1)] = lu_ref[...][None]
+    wt_ref[...] = jnp.dot(perm[...], wv[...], preferred_element_type=F32).T.astype(BF16)
     acc[...] = jnp.zeros_like(acc)
 
     pos_i = lax.broadcasted_iota(jnp.int32, (ni, nj), 0) + me * ni
@@ -155,15 +197,16 @@
                     if t < steps(way, ph):
                         ring(way, ph, t + 1, kind).start()
 
-    free_rows = lbu.shape[0] * lbu.shape[1]
-    block_rows = 128
+    free_rows = ltu.shape[1]
 
     def left_ready():
         for k in range(1, ncol):
             for kind in (0, 1):
                 left_copy(k, kind, True).wait_recv()
-        ltp[...] = lbp[...].reshape(-1, ni * chans).T
-        ltu[...] = lbu[...].reshape(-1, ni * chans).T
+        for k in range(1, ncol):
+            for kind in (0, 1):
+                left_copy(k, kind, False).wait_send()
+        ltp[...] = lbp[...].reshape(-1, tall).T
 
         def mask_rows(b, _):
             rows = pl.ds(pl.multiple_of(b * block_rows, block_rows), block_rows)
@@ -204,62 +247,72 @@
             acc[:, to] += jnp.dot(w, x, preferred_element_type=F32)
 
     units = ni // ROWS_PER_UNIT
-    for t in range(1, half + 1):
-        for ph in (0, 1):
-            forward(ph, t)
-            if t == half:
-                pass
-        if t == half - 1:
-            first_sends((2, 3))
-        if t == half // 2:
+
+    def work(ph, lo, hi):
+        def one(n, _):
+            unit(ph, n)
+            return 0
+
+        lax.fori_loop(lo, hi, one, 0)
+
+    plan = {
+        9: ((0, 0, 4),),
+        10: ((0, 4, 8),),
+        11: ((1, 0, 6),),
+        12: ((1, 6, 8), (2, 0, 3)),
+        13: ((2, 3, 8),),
+    }
+    for slot in range(1, half + STAGGER * (PHASES - 1) + 1):
+        for ph in range(PHASES):
+            t = slot - STAGGER * ph
+            if 1 <= t <= half:
+                forward(ph, t)
+            if t == 0:
+                first_sends(ph)
+        if slot == half // 2 + 1:
             left_ready()
-    for t in range(1, half + 1):
-        for ph in (2, 3):
-            forward(ph, t)
-
-        def two(n, _, t=t):
-            unit(0, n + (t - 1))
-            unit(1, n + (t - 1))
-            return 0
-
-        lax.fori_loop(0, 1, two, 0)
+        for ph, lo, hi in plan.get(slot, ()):
+            work(ph, lo, hi)
+
+    hj = nj // nseq
+    rows_of = ROWS_PER_UNIT
+
+    def swap(n):
+        at = pl.ds(n * rows_of, rows_of)
+        return pltpu.make_async_remote_copy(
+            src_ref=part.at[at, pl.ds(pl.multiple_of(other * hj, hj), hj), :],
+            dst_ref=got.at[at],
+            send_sem=send_x.at[n],
+            recv_sem=recv_x.at[n],
+            device_id={"seq": other},
+            device_id_type=MESH,
+        )
+
+    def finish(n):
+        swap(n).wait_recv()
+        at = pl.ds(n * rows_of, rows_of)
+        mine = part[at, pl.ds(pl.multiple_of(seq * hj, hj), hj), :]
+        out_ref[at] = (mine + got[at] + bias_ref[...][None]).astype(BF16)
 
     def tail(n, _):
-        unit(2, n)
-        unit(3, n)
+        unit(PHASES - 1, n)
+        for ii in range(rows_of):
+            i = n * rows_of + ii
+            tile = acc[:, pl.ds(pl.multiple_of(i * nj, nj), nj)] * scale_ref[pl.ds(i, 1), :]
+            part[pl.ds(i, 1)] = tile.T[None]
+        swap(n).start()
+
+        @pl.when(n >= 2)
+        def _():
+            finish(n - 2)
+
         return 0
 
     lax.fori_loop(0, units, tail, 0)
-
-    def turn(i, _):
-        tile = acc[:, pl.ds(pl.multiple_of(i * nj, nj), nj)] * scale_ref[pl.ds(i, 1), :]
-        part[pl.ds(i, 1)] = tile.T[None]
-        return 0
-
-    lax.fori_loop(0, ni, turn, 0)
-    hj = nj // nseq
-    swap = pltpu.make_async_remote_copy(
-        src_ref=part.at[:, pl.ds(pl.multiple_of(other * hj, hj), hj), :],
-        dst_ref=got,
-        send_sem=send_x,
-        recv_sem=recv_x,
-        device_id={"seq": other},
-        device_id_type=MESH,
-    )
-    swap.start()
-    swap.wait_recv()
-
-    def finish(i, _):
-        mine = part[pl.ds(i, 1), pl.ds(pl.multiple_of(seq * hj, hj), hj), :]
-        out_ref[pl.ds(i, 1)] = (mine + got[pl.ds(i, 1)] + bias_ref[...][None]).astype(BF16)
-        return 0
-
-    lax.fori_loop(0, ni, finish, 0)
-
-    swap.wait_send()
-    for k in range(1, ncol):
-        for kind in (0, 1):
-            left_copy(k, kind, False).wait_send()
+    finish(units - 2)
+    finish(units - 1)
+    for n in range(units):
+        swap(n).wait_send()
     for ph in range(PHASES):
         for way in (0, 1):
             for t in range(1, steps(way, ph) + 1):
@@ -272,30 +325,33 @@
     chans, ni = pl_.shape[1], pl_.shape[2]
     nj = pr.shape[2]
     nz = weight.shape[1]
-    rp = pr.reshape(pr.shape[0], chans * nj)
-    ru = ur.reshape(ur.shape[0], chans * nj)
-    lp = jnp.transpose(pl_, (0, 2, 1)).reshape(pl_.shape[0], ni * chans)
-    lu = jnp.transpose(ul, (0, 2, 1)).reshape(ul.shape[0], ni * chans)
-    wt = jnp.transpose(weight.reshape(chans, chans, nz), (2, 1, 0)).reshape(nz, chans * chans)
     s_paired = float(pr.shape[0] * nrow * nseq)
     dims = (nrow, ncol, nseq, chans, lengths.shape[0], ni, nj, nz, s_paired)
     half = nrow // 2
+    tall = ni * chans
     vm = pl.BlockSpec(memory_space=pltpu.VMEM)
+    hbm = pl.BlockSpec(memory_space=pltpu.HBM)
     sm = pl.BlockSpec(memory_space=pltpu.SMEM)
     dma = pltpu.SemaphoreType.DMA
     hj = nj // nseq
     return pl.pallas_call(
         functools.partial(kernel, dims),
         out_shape=jax.ShapeDtypeStruct((ni, hj, nz), BF16),
-        in_specs=[vm] * 6 + [sm] * 2,
+        in_specs=[hbm] * 5 + [vm] + [sm] * 2,
         out_specs=vm,
         scratch_shapes=[
+            pltpu.VMEM(pr.shape, BF16),
+            pltpu.VMEM(ur.shape, BF16),
+            pltpu.VMEM((chans, ni, pl_.shape[0]), BF16),
+            pltpu.VMEM((chans, ni, ul.shape[0]), BF16),
+            pltpu.VMEM(weight.shape, BF16),
+            pltpu.VMEM((tall, tall), BF16),
+            pltpu.VMEM((nz, tall), BF16),
             pltpu.VMEM((nrow, pr.shape[0], chans * nj), BF16),
             pltpu.VMEM((nrow, ur.shape[0], chans * nj), BF16),
-            pltpu.VMEM((ncol, *lp.shape), BF16),
-            pltpu.VMEM((ncol, *lu.shape), BF16),
-            pltpu.VMEM((ni * chans, ncol * lp.shape[0]), BF16),
-            pltpu.VMEM((ni * chans, ncol * lu.shape[0]), BF16),
+            pltpu.VMEM((ncol, pl_.shape[0], tall), BF16),
+            pltpu.VMEM((tall, ncol * pl_.shape[0]), BF16),
+            pltpu.VMEM((tall, ncol * ul.shape[0]), BF16),
             pltpu.VMEM((nz, ni * nj), F32),
             pltpu.VMEM((ni, nj, nz), F32),
             pltpu.VMEM((ni, hj, nz), F32),
@@ -305,13 +361,23 @@
             dma((2 * PHASES * half * 2,)),
             dma(((ncol - 1) * 2,)),
             dma(((ncol - 1) * 2,)),
-            dma,
-            dma,
+            dma((ni // ROWS_PER_UNIT,)),
+            dma((ni // ROWS_PER_UNIT,)),
+            dma((5,)),
         ],
         compiler_params=pltpu.CompilerParams(
-            collective_id=0, has_side_effects=True, vmem_limit_bytes=48 * 1024 * 1024
+            collective_id=0, has_side_effects=True, vmem_limit_bytes=67043328
         ),
-    )(rp, ru, lp, lu, wt, bias.reshape(1, nz), lengths, depths)
+    )(
+        pr,
+        ur,
+        jnp.transpose(pl_, (1, 2, 0)),
+        jnp.transpose(ul, (1, 2, 0)),
+        weight,
+        bias.reshape(1, nz),
+        lengths,
+        depths,
+    )
 
 
 def solution(mesh):

time: 118 us -> 113 us (0.958)
  local copies, waits for them, and re-layouts: 5.6 us -> 1.87 us
    unnamed x18 -> x1, local copies, waits for them, and re-layouts: 4.97 us -> 1.87 us
    pallas_call x1, Pallas kernels: 112 us -> 111 us  [body(): pl.pallas_call(functools.partial(kernel, dims), out_shape=jax.ShapeDtypeS...]
where the time goes in v2:
time: 113 us
  Pallas kernels  111 us (98%)
  local copies, waits for them, and re-layouts  1.87 us (2%)
    pallas_call x1, Pallas kernels, body(): pl.pallas_call(functools.partial(kernel, dims), out_shape=jax.ShapeDtypeS...  111 us

profile of v2, /device:TPU:33, one launch (start us, length us, event | category | flops | bytes accessed | tf_op | source)
XLA Modules:
  0.0 112.5 jit_solution(16465521801997921341)
XLA Ops:
  0.0 110.6 %shard_map.82 = bf16[32,64,128]{2,1,0:T(8,128)(2,1)} custom-call(bf16[16,32,128]{2,1,0:T(8,128)(2,1)} %pr_ref.1, bf16[32,32,128]{2,1,0:T(8,128)(2,1)} %ur_ref.1, bf16[32,32,64]{2,1,0:T(8,128)(2,1)} %bitcast.3, bf16[32,32,128]{2,1,0:T(8,128)(2,1)} %bitcast.4, bf16[1024,128]{1,0:T(8,128)(2,1)} %w_ref.1, f32[1,128]{1,0:T(1,128)} %bitcast.5, s32[12]{0:T(128)} %len_ref.1, ...), custom_call_target="tpu_custom_call" | custom-call | tf_op jit(solution)/shard_map/pallas_call | solution.py:337
  110.6 1.9 %copy.10 = bf16[32,64,128]{2,1,0:T(8,128)(2,1)} copy(bf16[32,64,128]{2,1,0:T(8,128)(2,1)} %shard_map.82) | data formatting | bytes 1048576

commit v3 on v2

--- a/solution.py
+++ b/solution.py
@@ -11,8 +11,8 @@
 F32 = jnp.float32
 BF16 = jnp.bfloat16
 PHASES = 4
-ROWS_PER_UNIT = 4
-STAGGER = 2
+I_UNIT = 16
+TAIL_UNIT = 8
 
 
 def kernel(
@@ -169,7 +169,6 @@
         for kind in (0, 1):
             left_copy(k, kind, False).start()
     wt_ref[...] = jnp.dot(perm[...], wv[...], preferred_element_type=F32).T.astype(BF16)
-    acc[...] = jnp.zeros_like(acc)
 
     pos_i = lax.broadcasted_iota(jnp.int32, (ni, nj), 0) + me * ni
     pos_j = lax.broadcasted_iota(jnp.int32, (ni, nj), 1) + col * nj
@@ -210,32 +209,33 @@
 
         def mask_rows(b, _):
             rows = pl.ds(pl.multiple_of(b * block_rows, block_rows), block_rows)
-            shape = (block_rows, free_rows)
+            shape = (block_rows, nj)
             pos = (lax.broadcasted_iota(jnp.int32, shape, 0) + b * block_rows) // chans + me * ni
             ids = lax.broadcasted_iota(jnp.int32, shape, 1) + seq * free_rows
             depth = jnp.zeros(shape, jnp.int32)
             for k in range(chains):
                 low = ends[k - 1] if k else 0
                 depth = jnp.where((pos >= low) & (pos < ends[k]), dep_ref[k], depth)
-            live = jnp.where(ids < depth, 1.0, 0.0).astype(BF16)
-            ltu[rows, :] = ltu[rows, :] * live
+            for at in range(0, free_rows, nj):
+                live = jnp.where(ids + at < depth, 1.0, 0.0).astype(BF16)
+                ltu[rows, at : at + nj] = ltu[rows, at : at + nj] * live
             return 0
 
         lax.fori_loop(0, ni * chans // block_rows, mask_rows, 0)
 
-    def unit(ph, ib):
-        rows = ROWS_PER_UNIT * chans
-        at = pl.ds(pl.multiple_of(ib * rows, rows), rows)
+    def unit(ph, base, count):
+        rows = count * chans
+        at = pl.ds(pl.multiple_of(base * chans, rows), rows)
         part_of = pl.ds(ph * lanes, lanes)
         kp = rbp.shape[0] * rbp.shape[1]
         ku = rbu.shape[0] * rbu.shape[1]
         a = jnp.dot(ltp[at, :], rbp[:, :, part_of].reshape(kp, lanes), preferred_element_type=F32)
         b = jnp.dot(ltu[at, :], rbu[:, :, part_of].reshape(ku, lanes), preferred_element_type=F32)
         w = wt_ref[:, ph * per_phase * chans : (ph + 1) * per_phase * chans]
-        for pair in range(ROWS_PER_UNIT // 2):
+        for pair in range(count // 2):
             cols = []
             for ii in (2 * pair, 2 * pair + 1):
-                m = same_ref[pl.ds(ib * ROWS_PER_UNIT + ii, 1), :]
+                m = same_ref[pl.ds(base + ii, 1), :]
                 tiles = []
                 for d in range(per_phase):
                     rs = slice(ii * chans, (ii + 1) * chans)
@@ -243,39 +243,40 @@
                     tiles.append((a[rs, ls] + b[rs, ls] * m).astype(BF16))
                 cols.append(jnp.concatenate(tiles, axis=0))
             x = jnp.concatenate(cols, axis=1)
-            to = pl.ds(pl.multiple_of((ib * ROWS_PER_UNIT + 2 * pair) * nj, 2 * nj), 2 * nj)
-            acc[:, to] += jnp.dot(w, x, preferred_element_type=F32)
-
-    units = ni // ROWS_PER_UNIT
-
-    def work(ph, lo, hi):
+            to = pl.ds(pl.multiple_of((base + 2 * pair) * nj, 2 * nj), 2 * nj)
+            y = jnp.dot(w, x, preferred_element_type=F32)
+            if ph == 0:
+                acc[:, to] = y
+            else:
+                acc[:, to] += y
+
+    def whole(ph):
         def one(n, _):
-            unit(ph, n)
+            unit(ph, n * I_UNIT, I_UNIT)
             return 0
 
-        lax.fori_loop(lo, hi, one, 0)
-
-    plan = {
-        9: ((0, 0, 4),),
-        10: ((0, 4, 8),),
-        11: ((1, 0, 6),),
-        12: ((1, 6, 8), (2, 0, 3)),
-        13: ((2, 3, 8),),
-    }
-    for slot in range(1, half + STAGGER * (PHASES - 1) + 1):
-        for ph in range(PHASES):
-            t = slot - STAGGER * ph
-            if 1 <= t <= half:
-                forward(ph, t)
-            if t == 0:
-                first_sends(ph)
-        if slot == half // 2 + 1:
+        lax.fori_loop(0, ni // I_UNIT, one, 0)
+
+    first_sends(1)
+    for t in range(1, half + 1):
+        for ph in (0, 1):
+            forward(ph, t)
+        if t == half - 1:
+            first_sends(2)
+            first_sends(3)
+        if t == half // 2:
             left_ready()
-        for ph, lo, hi in plan.get(slot, ()):
-            work(ph, lo, hi)
+    for t in range(1, half + 1):
+        for ph in (2, 3):
+            forward(ph, t)
+            if t == half and ph == 2:
+                whole(2)
+        if t in (1, 2):
+            whole(t - 1)
 
     hj = nj // nseq
-    rows_of = ROWS_PER_UNIT
+    rows_of = TAIL_UNIT
+    units = ni // rows_of
 
     def swap(n):
         at = pl.ds(n * rows_of, rows_of)
@@ -295,21 +296,20 @@
         out_ref[at] = (mine + got[at] + bias_ref[...][None]).astype(BF16)
 
     def tail(n, _):
-        unit(PHASES - 1, n)
+        unit(PHASES - 1, n * rows_of, rows_of)
         for ii in range(rows_of):
             i = n * rows_of + ii
             tile = acc[:, pl.ds(pl.multiple_of(i * nj, nj), nj)] * scale_ref[pl.ds(i, 1), :]
             part[pl.ds(i, 1)] = tile.T[None]
         swap(n).start()
 
-        @pl.when(n >= 2)
+        @pl.when(n >= 1)
         def _():
-            finish(n - 2)
+            finish(n - 1)
 
         return 0
 
     lax.fori_loop(0, units, tail, 0)
-    finish(units - 2)
     finish(units - 1)
     for n in range(units):
         swap(n).wait_send()
@@ -361,12 +361,12 @@
             dma((2 * PHASES * half * 2,)),
             dma(((ncol - 1) * 2,)),
             dma(((ncol - 1) * 2,)),
-            dma((ni // ROWS_PER_UNIT,)),
-            dma((ni // ROWS_PER_UNIT,)),
+            dma((ni // TAIL_UNIT,)),
+            dma((ni // TAIL_UNIT,)),
             dma((5,)),
         ],
         compiler_params=pltpu.CompilerParams(
-            collective_id=0, has_side_effects=True, vmem_limit_bytes=67043328
+            collective_id=0, has_side_effects=True, vmem_limit_bytes=67043328 - 600 * 1024
         ),
     )(
         pr,

time: 113 us -> 109 us (0.965)
  Pallas kernels: 111 us -> 107 us
    pallas_call x1, Pallas kernels: 111 us -> 107 us  [body(): pl.pallas_call(functools.partial(kernel, dims), out_shape=jax.ShapeDtypeS...]
where the time goes in v3:
time: 109 us
  Pallas kernels  107 us (98%)
  local copies, waits for them, and re-layouts  1.87 us (2%)
    pallas_call x1, Pallas kernels, body(): pl.pallas_call(functools.partial(kernel, dims), out_shape=jax.ShapeDtypeS...  107 us

profile of v3, /device:TPU:33, one launch (start us, length us, event | category | flops | bytes accessed | tf_op | source)
XLA Modules:
  0.0 108.6 jit_solution(13199403445881280843)
XLA Ops:
  0.0 106.8 %shard_map.82 = bf16[32,64,128]{2,1,0:T(8,128)(2,1)} custom-call(bf16[16,32,128]{2,1,0:T(8,128)(2,1)} %pr_ref.1, bf16[32,32,128]{2,1,0:T(8,128)(2,1)} %ur_ref.1, bf16[32,32,64]{2,1,0:T(8,128)(2,1)} %bitcast.3, bf16[32,32,128]{2,1,0:T(8,128)(2,1)} %bitcast.4, bf16[1024,128]{1,0:T(8,128)(2,1)} %w_ref.1, f32[1,128]{1,0:T(1,128)} %bitcast.5, s32[12]{0:T(128)} %len_ref.1, ...), custom_call_target="tpu_custom_call" | custom-call | tf_op jit(solution)/shard_map/pallas_call | solution.py:337
  106.8 1.9 %copy.10 = bf16[32,64,128]{2,1,0:T(8,128)(2,1)} copy(bf16[32,64,128]{2,1,0:T(8,128)(2,1)} %shard_map.82) | data formatting | bytes 1048576

commit v4 on v3

--- a/solution.py
+++ b/solution.py
@@ -144,6 +144,7 @@
         )
 
     first_sends(0)
+    first_sends(1)
 
     block_rows = 128
 
@@ -257,22 +258,23 @@
 
         lax.fori_loop(0, ni // I_UNIT, one, 0)
 
-    first_sends(1)
-    for t in range(1, half + 1):
-        for ph in (0, 1):
-            forward(ph, t)
-        if t == half - 1:
+    lag = 2
+    for slot in range(1, half + lag + 1):
+        for ph in range(PHASES):
+            t = slot - (lag if ph >= 2 else 0)
+            if 1 <= t <= half:
+                forward(ph, t)
+            if slot == half + lag and ph == 2:
+                whole(2)
+        if slot == lag:
             first_sends(2)
             first_sends(3)
-        if t == half // 2:
+        if slot == half // 2:
             left_ready()
-    for t in range(1, half + 1):
-        for ph in (2, 3):
-            forward(ph, t)
-            if t == half and ph == 2:
-                whole(2)
-        if t in (1, 2):
-            whole(t - 1)
+        if slot == half:
+            whole(0)
+        if slot == half + 1:
+            whole(1)
 
     hj = nj // nseq
     rows_of = TAIL_UNIT

time: 109 us -> 106 us (0.972)
  Pallas kernels: 107 us -> 104 us
    pallas_call x1, Pallas kernels: 107 us -> 104 us  [body(): pl.pallas_call(functools.partial(kernel, dims), out_shape=jax.ShapeDtypeS...]
where the time goes in v4:
time: 106 us
  Pallas kernels  104 us (98%)
  local copies, waits for them, and re-layouts  1.87 us (2%)
    pallas_call x1, Pallas kernels, body(): pl.pallas_call(functools.partial(kernel, dims), out_shape=jax.ShapeDtypeS...  104 us

profile of v4, /device:TPU:33, one launch (start us, length us, event | category | flops | bytes accessed | tf_op | source)
XLA Modules:
  0.0 105.7 jit_solution(13920021993863078724)
XLA Ops:
  0.0 103.8 %shard_map.82 = bf16[32,64,128]{2,1,0:T(8,128)(2,1)} custom-call(bf16[16,32,128]{2,1,0:T(8,128)(2,1)} %pr_ref.1, bf16[32,32,128]{2,1,0:T(8,128)(2,1)} %ur_ref.1, bf16[32,32,64]{2,1,0:T(8,128)(2,1)} %bitcast.3, bf16[32,32,128]{2,1,0:T(8,128)(2,1)} %bitcast.4, bf16[1024,128]{1,0:T(8,128)(2,1)} %w_ref.1, f32[1,128]{1,0:T(1,128)} %bitcast.5, s32[12]{0:T(128)} %len_ref.1, ...), custom_call_target="tpu_custom_call" | custom-call | tf_op jit(solution)/shard_map/pallas_call | solution.py:339
  103.8 1.9 %copy.10 = bf16[32,64,128]{2,1,0:T(8,128)(2,1)} copy(bf16[32,64,128]{2,1,0:T(8,128)(2,1)} %shard_map.82) | data formatting | bytes 1048576

commit v5 on v4

--- a/solution.py
+++ b/solution.py
@@ -11,7 +11,7 @@
 F32 = jnp.float32
 BF16 = jnp.bfloat16
 PHASES = 4
-I_UNIT = 16
+I_UNIT = 32
 TAIL_UNIT = 8
 
 
@@ -258,7 +258,7 @@
 
         lax.fori_loop(0, ni // I_UNIT, one, 0)
 
-    lag = 2
+    lag = 3
     for slot in range(1, half + lag + 1):
         for ph in range(PHASES):
             t = slot - (lag if ph >= 2 else 0)

time: 106 us -> 106 us (level)
  no operation moved by 1% of the time
where the time goes in v5:
time: 106 us; the launch traced here: 105 us
  Pallas kernels  103 us (97%)
  local copies, waits for them, and re-layouts  1.87 us (2%)
    pallas_call x1, Pallas kernels, body(): pl.pallas_call(functools.partial(kernel, dims), out_shape=jax.ShapeDtypeS...  103 us

profile of v5, /device:TPU:33, one launch (start us, length us, event | category | flops | bytes accessed | tf_op | source)
XLA Modules:
  0.0 105.3 jit_solution(8718004134782674578)
XLA Ops:
  0.0 103.5 %shard_map.82 = bf16[32,64,128]{2,1,0:T(8,128)(2,1)} custom-call(bf16[16,32,128]{2,1,0:T(8,128)(2,1)} %pr_ref.1, bf16[32,32,128]{2,1,0:T(8,128)(2,1)} %ur_ref.1, bf16[32,32,64]{2,1,0:T(8,128)(2,1)} %bitcast.3, bf16[32,32,128]{2,1,0:T(8,128)(2,1)} %bitcast.4, bf16[1024,128]{1,0:T(8,128)(2,1)} %w_ref.1, f32[1,128]{1,0:T(1,128)} %bitcast.5, s32[12]{0:T(128)} %len_ref.1, ...), custom_call_target="tpu_custom_call" | custom-call | tf_op jit(solution)/shard_map/pallas_call | solution.py:339
  103.5 1.9 %copy.10 = bf16[32,64,128]{2,1,0:T(8,128)(2,1)} copy(bf16[32,64,128]{2,1,0:T(8,128)(2,1)} %shard_map.82) | data formatting | bytes 1048576
